TPU v7x, 32 devices: a whole 2x2x4 slice. The times are simulated.
32 devices in a mesh: member: 2 (over x), node: 16 (over z, y, core).
Axes of the slice: x: 2, y: 2, z: 4, core: 2. Of those that a mesh axis runs over, the one named last changes fastest.
Arguments:
- conditioning: bfloat16 [168, 32768], P(None, ('member', 'node')), parts along dimension 1, may hold values from -6 to 6
- target_state: float32 [84, 32768], P(None, ('member', 'node')), parts along dimension 1, may hold values from -6 to 6
- noise_sample: float32 [84, 32768], P(None, ('member', 'node')), parts along dimension 1, may hold values from -6 to 6
- step_index: int32 [2], P('member'), parts along dimension 0, may hold values from 0 to 19
- mesh_features: float32 [3, 10240], P(None, 'node'), may hold values from -1 to 1
- edge_geometry: float32 [4, 65536], P(None, 'node'), may hold values from -6 to 6
- edge_slot: int32 [65536], P('node'), may hold values from 0 to 255, as said below
- edge_receiver: int32 [65536], P('node'), may hold values from 0 to 639
- send_rows: int32 [256, 16], P('node'), may hold values from 0 to 1023
- edge_count: int32 [16], P('node'), may hold values from 1399 to 4096, as said below
- embed_weight: bfloat16 [252, 512], replicated, may hold values from -0.375 to 0.375
- mesh_weight: float32 [3, 512], replicated, may hold values from -3.5 to 3.5
- geom_weight: float32 [4, 512], replicated, may hold values from -3 to 3
- sender_weight: bfloat16 [512, 512], P('node'), may hold values from -0.15625 to 0.15625
- edge_weight: bfloat16 [512, 512], P('node'), may hold values from -0.15625 to 0.15625
- receiver_weight: bfloat16 [512, 512], P('node'), may hold values from -0.15625 to 0.15625
- message_weight: bfloat16 [512, 512], P('node'), may hold values from -0.25 to 0.25
- node_weight: bfloat16 [1024, 512], P('node'), may hold values from -0.1875 to 0.1875
- output_weight: bfloat16 [512, 512], P('node'), may hold values from -0.25 to 0.25
- noise_weight: float32 [32, 512], replicated, may hold values from -1 to 1
- film_weight: bfloat16 [512, 2048], replicated, may hold values from -0.25 to 0.25
Outputs:
- mesh_latent: bfloat16 [10240, 1024], P('node', 'member'), parts along dimension 1
There are 2 independent parts, one for each index of `member`. A program takes and returns all parts, laid end to end along the dimension named above; an argument that names none is the same for every part. Nothing has to cross between parts.
Inputs may be any that keep to these rules, and one draw needn't show every extreme that they name: `edge_slot`: on each device, the live slots name every entry of its 16 * 16 list at least once, or as many distinct entries as there are live slots where these are fewer. `edge_count`: the counts sum to 16 * 2048 and one device has all 4096 slots live.
All inputs are finite; a program needn't handle non-finite values.
Results may differ from a plain program's by a relative error of at most 0.0071.
Values may be sent and summed in bfloat16 or wider, within the bound.
A program may use at most 64 MiB of HBM per device.

v0:
```python
import functools

import jax
import jax.numpy as jnp
from jax import lax
from jax.experimental import pallas as pl
from jax.experimental.pallas import tpu as pltpu
from jax.sharding import PartitionSpec as P

STEPS = 20


sigma_top = 80.0
sigma_low = 0.03
rho_power = 7.0
norm_eps = 1e-05
f32, bf16 = jnp.float32, jnp.bfloat16


def is_folded(mesh):
    rows = mesh.devices[0]
    places = [getattr(device, "coords", None) for device in rows[:5:2]]
    if len(places) < 3 or any(place is None for place in places):
        return False
    first = [a != b for a, b in zip(places[0], places[1])]
    second = [a != b for a, b in zip(places[0], places[2])]
    return first != second


def silu(x):
    half = 0.5 * x
    return half * jnp.tanh(half) + half


def outer_sum(columns, rows):
    total = columns[:, 0:1] * rows[0:1, :]
    for index in range(1, rows.shape[0]):
        total = total + columns[:, index : index + 1] * rows[index : index + 1, :]
    return total


def normalised(values):
    mean = jnp.mean(values, axis=0, keepdims=True)
    centred = values - mean
    var = jnp.mean(centred * centred, axis=0, keepdims=True)
    return centred * lax.rsqrt(var + norm_eps)


def nn(a, b):
    return jnp.dot(a, b, preferred_element_type=f32)


def nt(a, b):
    return lax.dot_general(a, b, (((1,), (1,)), ((), ())), preferred_element_type=f32)


def encoder_kernel(n, folded, block, *refs):
    step_ref, count_ref, slot_ref, recv_ref, rows_ref, geom_ref, mesh_ref = refs[:7]
    cond_ref, target_ref, noise_ref, embed_ref, mesh_w_ref, geom_w_ref, noise_w_ref, film_w_ref = refs[7:15]
    shards, out_ref = refs[15:21], refs[21]
    fulls = refs[22:28]
    picked_ref, outgoing, arrived, embed_pad_ref, cols_ref, edges_ref = refs[28:34]
    table_ref, edge_t_ref, message_t_ref, embed_t_ref, total_ref = refs[34:39]
    send_sem, recv_sem, psend_sem, precv_sem, asend_sem, arecv_sem, own_sem = refs[39:]
    me = lax.axis_index("node")
    core, chip = me % 2, me // 2
    partner = chip * 2 + 1 - core
    chips = n // 2
    half = chips // 2

    def same(index):
        return index

    if folded:

        def to_pos(c):
            z, y = c // 2, c % 2
            return z + y * (chips - 1 - 2 * z)

        def to_chip(p):
            y = p // half
            return (p + y * (chips - 1 - 2 * p)) * 2 + y
    else:
        to_pos = to_chip = same

    pos = to_pos(chip)

    def device_at(shift):
        return to_chip((pos + shift + chips) % chips) * 2 + core

    sent = []

    def remote(source, target, send, recv, device):
        copy = pltpu.make_async_remote_copy(
            src_ref=source, dst_ref=target, send_sem=send, recv_sem=recv, device_id={"node": device}
        )
        copy.start()
        sent.append(copy)
        return copy

    long, short = chips // 2, chips - 1 - chips // 2
    reach = [[long, short] if k % 2 == 0 else [short, long] for k in range(6)]
    ring = {}
    passed = {k: [] for k in range(6)}
    early, late = (0, 1, 2, 3), (4, 5)

    def relay(group, step):
        onward = []
        for k in group:
            for side in (0, 1):
                way = 1 - 2 * side
                last = reach[k][side]
                if step > last + 1:
                    continue
                block_at = device_at(-way * (step - 1))
                target = fulls[k].at[block_at]
                source = shards[k] if step == 1 else target
                if step > 1:
                    ring[k, side, step - 1].wait_recv()
                if step <= last:
                    ring[k, side, step] = remote(
                        source,
                        target,
                        send_sem.at[k, side, step],
                        recv_sem.at[k, side, step],
                        device_at(way),
                    )
                if step > 1 or side == 0:
                    index = side * (long + 1) + step - 1
                    onward.append((k, index, source, target))
        for k, index, source, target in onward:
            passed[k].append(
                remote(source, target, psend_sem.at[k, index], precv_sem.at[k, index], partner)
            )

    barrier = pltpu.get_barrier_semaphore()
    for step in range(1, n):
        pl.semaphore_signal(barrier, inc=1, device_id={"node": (me + step) % n})
    own = []
    for k in range(6):
        own.append(pltpu.make_async_copy(shards[k], fulls[k].at[me], own_sem.at[k]))
        own[k].start()
    pl.semaphore_wait(barrier, n - 1)
    relay(early, 1)

    width = embed_ref.shape[1]
    channels = embed_ref.shape[0]
    cap = outgoing.shape[1]
    frac = jnp.full((1, 1), step_ref[0], jnp.int32).astype(f32) / (STEPS - 1)
    upper = sigma_top ** (1.0 / rho_power)
    lower = sigma_low ** (1.0 / rho_power)
    root = upper + frac * (lower - upper)
    cube = root * root * root
    sigma = cube * cube * root
    noisy = ((target_ref[...] + sigma * noise_ref[...]) / jnp.sqrt(sigma * sigma + 1.0)).astype(bf16)
    points, listed = cond_ref.shape[1], rows_ref.shape[1]
    fixed = cond_ref.shape[0]
    pick = lax.broadcasted_iota(jnp.int32, (points, listed), 0) == rows_ref[...]
    pick = pick.astype(f32).astype(bf16)
    picked_ref[...] = jnp.zeros_like(picked_ref)
    picked_ref[:fixed, :] = nn(cond_ref[...], pick)
    picked_ref[fixed:channels, :] = nn(noisy, pick)
    outgoing[...] = picked_ref[...].T.astype(bf16).reshape(outgoing.shape)
    relay(early, 2)

    freqs = noise_w_ref.shape[0] // 2
    place_k = lax.broadcasted_iota(jnp.int32, (2 * freqs, 1), 0)
    wave = (place_k % freqs + 1).astype(f32)
    angle = 0.25 * jnp.log(sigma) * wave
    fourier = jnp.where(place_k < freqs, jnp.sin(angle), jnp.cos(angle))
    cond = silu(jnp.sum(fourier * noise_w_ref[...], axis=0, keepdims=True)).astype(bf16)
    film = nn(cond, film_w_ref[...])
    small = [film[:, width * i : width * (i + 1)] for i in range(4)]
    geoms, feats = geom_w_ref.shape[0], mesh_w_ref.shape[0]
    small += [geom_w_ref[i : i + 1, :] for i in range(geoms)]
    small += [mesh_w_ref[i : i + 1, :] for i in range(feats)]
    line = lax.broadcasted_iota(jnp.int32, (128, width), 0)
    stacked = jnp.zeros((128, width), f32)
    for i, row in enumerate(small):
        stacked = jnp.where(line == i, row, stacked)
    cols_ref[...] = stacked.T
    geom_cols = cols_ref[:, 4 : 4 + geoms]
    mesh_cols = cols_ref[:, 4 + geoms : 4 + geoms + feats]
    mesh_embed = silu(outer_sum(mesh_cols, mesh_ref[...])).astype(bf16)
    embed_t_ref[...] = mesh_embed

    own.append(pltpu.make_async_copy(outgoing.at[me], arrived.at[me], own_sem.at[6]))
    own[6].start()
    swaps = []
    for step in range(1, n):
        other = (me + step) % n
        swaps.append(
            remote(outgoing.at[other], arrived.at[me], asend_sem.at[step], arecv_sem.at[step], other)
        )
    relay(early, 3)
    relay(late, 1)

    blocks = geom_ref.shape[1] // block

    def embed_edges(index, carry):
        here = pl.ds(pl.multiple_of(index * block, block), block)
        edges_ref[index] = silu(outer_sum(geom_cols, geom_ref[:, here])).astype(bf16)
        return carry

    lax.fori_loop(0, blocks // 2, embed_edges, 0)
    relay(early, 4)
    lax.fori_loop(blocks // 2, blocks, embed_edges, 0)
    for step in range(5, long + 2):
        relay(early, step)
    embed_pad_ref[...] = jnp.zeros_like(embed_pad_ref)
    embed_pad_ref[:channels, :] = embed_ref[...]
    for copy in own:
        copy.wait()
    for copy in swaps:
        copy.wait_recv()
    sources = arrived[...].reshape(listed, arrived.shape[2])
    received = silu(nt(embed_pad_ref[...].T, sources)).astype(bf16)

    def full(k):
        return fulls[k][...].reshape(-1, width)

    for k in early:
        for copy in passed[k]:
            copy.wait_recv()
    table_ref[:, :listed] = nn(full(0).T, received).astype(bf16)
    edge_t_ref[...] = full(1).T
    table_ref[:, listed:] = nn(full(2).T, embed_t_ref[...]).astype(bf16)
    message_t_ref[...] = full(3).T
    total_ref[...] = jnp.zeros_like(total_ref)
    nodes = mesh_ref.shape[1]
    count = count_ref[0]

    def add_block(index, carry):
        start = pl.multiple_of(index * block, block)
        here = pl.ds(start, block)
        recv = recv_ref[:, here]
        live = start + lax.broadcasted_iota(jnp.int32, (1, block), 1) < count
        recv = jnp.where(live, recv, -1)
        pick = lax.broadcasted_iota(jnp.int32, (listed, block), 0) == slot_ref[:, here]
        pick = pick.astype(f32).astype(bf16)
        place = lax.broadcasted_iota(jnp.int32, (nodes, block), 0) == recv
        place = place.astype(f32).astype(bf16)
        pre = nn(edge_t_ref[...], edges_ref[index])
        pre = pre + nn(table_ref[:, :listed], pick)
        pre = pre + nn(table_ref[:, listed:], place)
        hidden = silu(pre).astype(bf16)
        mixed = nn(message_t_ref[...], hidden)
        message = normalised(mixed) * (1.0 + cols_ref[:, 0:1]) + cols_ref[:, 1:2]
        total_ref[...] += nt(message.astype(bf16), place)
        return carry

    stages = min(long, blocks)
    for stage in range(stages):
        lax.fori_loop(blocks * stage // stages, blocks * (stage + 1) // stages, add_block, 0)
        relay(late, stage + 2)
    for step in range(stages + 2, long + 2):
        relay(late, step)
    for k in late:
        for copy in passed[k]:
            copy.wait_recv()
    node_t = full(4).T
    update = nn(node_t[:, :width], embed_t_ref[...])
    update = update + nn(node_t[:, width:], total_ref[...].astype(bf16))
    update = silu(update).astype(bf16)
    result = nn(full(5).T, update)
    result = normalised(result) * (1.0 + cols_ref[:, 2:3]) + cols_ref[:, 3:4]
    out_ref[...] = (embed_t_ref[...].astype(f32) + result).T.astype(bf16)
    for copy in sent:
        copy.wait_send()


def per_device(n, folded, *args):
    conditioning, target_state, noise_sample, step_index, mesh_features, edge_geometry = args[:6]
    edge_slot, edge_receiver, send_rows, edge_count, embed_weight, mesh_weight, geom_weight = args[6:13]
    shards, noise_weight, film_weight = args[13:19], args[19], args[20]
    channels, width = embed_weight.shape
    nodes, edges = mesh_features.shape[1], edge_geometry.shape[1]
    cap = send_rows.shape[1]
    listed = n * cap
    deep = channels + -channels % 128
    block = min(512, edges)
    long = n // 4 + 1
    dma = pltpu.SemaphoreType.DMA
    vmem = pl.BlockSpec(memory_space=pltpu.VMEM)
    smem = pl.BlockSpec(memory_space=pltpu.SMEM)
    return pl.pallas_call(
        functools.partial(encoder_kernel, n, folded, block),
        out_shape=jax.ShapeDtypeStruct((nodes, width), bf16),
        in_specs=[smem] * 2 + [vmem] * 19,
        out_specs=vmem,
        scratch_shapes=[pltpu.VMEM((n,) + shard.shape, bf16) for shard in shards]
        + [
            pltpu.VMEM((deep, listed), f32),
            pltpu.VMEM((n, cap, deep), bf16),
            pltpu.VMEM((n, cap, deep), bf16),
            pltpu.VMEM((deep, width), bf16),
            pltpu.VMEM((width, 128), f32),
            pltpu.VMEM((edges // block, width, block), bf16),
            pltpu.VMEM((width, listed + nodes), bf16),
            pltpu.VMEM((width, width), bf16),
            pltpu.VMEM((width, width), bf16),
            pltpu.VMEM((width, nodes), bf16),
            pltpu.VMEM((width, nodes), f32),
            dma((6, 2, long + 1)),
            dma((6, 2, long + 1)),
            dma((6, 2 * (long + 1))),
            dma((6, 2 * (long + 1))),
            dma((n,)),
            dma((n,)),
            dma((7,)),
        ],
        compiler_params=pltpu.CompilerParams(collective_id=0, has_side_effects=True),
    )(
        step_index,
        edge_count,
        edge_slot.reshape(1, -1),
        edge_receiver.reshape(1, -1),
        send_rows.reshape(1, -1),
        edge_geometry,
        mesh_features,
        conditioning,
        target_state,
        noise_sample,
        embed_weight,
        mesh_weight,
        geom_weight,
        noise_weight,
        film_weight,
        *shards,
    )


def solution(mesh):
    placed = (
        P(None, ("member", "node")),
        P(None, ("member", "node")),
        P(None, ("member", "node")),
        P("member"),
        P(None, "node"),
        P(None, "node"),
        P("node"),
        P("node"),
        P("node", None),
        P("node"),
        P(),
        P(),
        P(),
        P("node", None),
        P("node", None),
        P("node", None),
        P("node", None),
        P("node", None),
        P("node", None),
        P(),
        P(),
    )
    n = mesh.shape["node"]
    body = functools.partial(per_device, n, is_folded(mesh))
    return jax.shard_map(
        body, mesh=mesh, in_specs=placed, out_specs=P("node", "member"), check_vma=False
    )
```

profile of v0, /device:TPU:0, one launch (start us, length us, event | category | flops | bytes accessed | tf_op | source)
XLA Modules:
  0.0 56.1 jit_solution(7495195195263041622)
XLA Ops:
  1.3 1.3 %reshape.11.refs_4_ = s32[1,256]{1,0:T(1,128)} reshape(s32[16,16]{1,0:T(8,128)} %param.29) | data formatting | bytes 2048 | tf_op jit(solution)/shard_map/reshape | solution.py:318
  2.6 51.4 %shard_map.199 = bf16[640,512]{1,0:T(8,128)(2,1)} custom-call(s32[1]{0:T(128)S(6)} %copy.23.refs_0_, s32[1]{0:T(128)S(6)} %copy.24.refs_1_, s32[1,4096]{1,0:T(1,128)} %bitcast.2, s32[1,4096]{1,0:T(1,128)} %bitcast.3, s32[1,256]{1,0:T(1,128)} %reshape.11.refs_4_, f32[4,4096]{1,0:T(4,128)} %refs_5_.1, f32[3,640]{1,0:T(4,128)} %refs_6_.1, ...), custom_call_target="tpu_custom_call" | custom-call | tf_op jit(solution)/shard_map/pallas_call | solution.py:286
  54.1 2.0 %copy.25 = bf16[640,512]{1,0:T(8,128)(2,1)} copy(bf16[640,512]{1,0:T(8,128)(2,1)} %shard_map.199) | data formatting | bytes 1310720
where the time goes:
time: 56.3 us; the launch traced here: 56.1 us
  Pallas kernels  51.4 us (91%)
  local copies, waits for them, and re-layouts  3.31 us (6%)
  between operations  1.31 us (2%)
    pallas_call x1, Pallas kernels, per_device(): pl.pallas_call(functools.partial(encoder_kernel, n, folded, block), out_s...  51.4 us
    unnamed x1, local copies, waits for them, and re-layouts  1.97 us
    reshape x1, local copies, waits for them, and re-layouts, per_device(): send_rows.reshape(1, -1)  1.34 us

commit v1 on v0

v1 whole, which is shorter than its diff:
```python
import functools

import jax
import jax.numpy as jnp
from jax import lax
from jax.experimental import pallas as pl
from jax.experimental.pallas import tpu as pltpu
from jax.sharding import PartitionSpec as P

STEPS = 20


sigma_top = 80.0
sigma_low = 0.03
rho_power = 7.0
norm_eps = 1e-05
f32, bf16 = jnp.float32, jnp.bfloat16


def is_folded(mesh):
    rows = mesh.devices[0]
    places = [getattr(device, "coords", None) for device in rows[:5:2]]
    if len(places) < 3 or any(place is None for place in places):
        return False
    first = [a != b for a, b in zip(places[0], places[1])]
    second = [a != b for a, b in zip(places[0], places[2])]
    return first != second


def silu(x):
    half = 0.5 * x
    return half * jnp.tanh(half) + half


def normalised(values):
    mean = jnp.mean(values, axis=1, keepdims=True)
    centred = values - mean
    var = jnp.mean(centred * centred, axis=1, keepdims=True)
    return centred * lax.rsqrt(var + norm_eps)


def nn(a, b):
    return jnp.dot(a, b, preferred_element_type=f32)


def nt(a, b):
    return lax.dot_general(a, b, (((1,), (1,)), ((), ())), preferred_element_type=f32)


def pieces(values):
    high = values.astype(bf16).astype(f32)
    rest = values - high
    middle = rest.astype(bf16).astype(f32)
    low = (rest - middle).astype(bf16).astype(f32)
    return high, middle, low


def stack_left(ref, values):
    a, b, c = pieces(values)
    ref[...] = jnp.zeros_like(ref)
    for i, part in enumerate((a, a, b, a, c, b)):
        ref[8 * i : 8 * i + values.shape[0], :] = part


def stack_right(ref, values):
    a, b, c = pieces(values)
    ref[...] = jnp.zeros_like(ref)
    for i, part in enumerate((a, b, a, c, a, b)):
        ref[8 * i : 8 * i + values.shape[0], :] = part


def encoder_kernel(n, members, folded, block, *refs):
    step_ref, count_ref = refs[:2]
    sources, shards, out_ref = refs[2:15], refs[15:21], refs[21]
    locals_, refs = refs[22:35], refs[35:]
    slot_ref, recv_ref, rows_ref, geom_ref, mesh_ref = locals_[:5]
    cond_ref, target_ref, noise_ref, embed_ref, mesh_w_ref, geom_w_ref, noise_w_ref, film_w_ref = locals_[5:]
    w_ref, raw_ref, pick_ref, outgoing, arrived, embed_pad_ref, turn_ref = refs[:7]
    mesh_s_ref, mesh_k_ref, geom_s_ref, geom_k_ref, nodes_ref, ohr_ref, ohs_ref = refs[7:14]
    place_ref, meshg_ref, edges_ref, pre_ref, table_ref, mixed_ref, total_ref = refs[14:21]
    z_send, z_recv, y_send, y_recv, x_send, x_recv, c_send, c_recv = refs[21:29]
    a_send, a_recv, in_sem, own_sem = refs[29:]
    me = lax.axis_index("node")
    member = lax.axis_index("member")
    wide = 2 if folded else 1
    deep = n // 2 // wide
    core, chip = me % 2, me // 2
    y, z = chip % wide, chip // wide
    paired = members % 2 == 0
    x = member % 2 if paired else 0
    other_member = member + 1 - 2 * x
    width = w_ref.shape[3]
    part = width // 2 if paired else width

    def node_at(zz, yy, cc):
        return (zz * wide + yy) * 2 + cc

    sent = []

    def remote(source, target, send, recv, device):
        copy = pltpu.make_async_remote_copy(
            src_ref=source, dst_ref=target, send_sem=send, recv_sem=recv, device_id=device
        )
        copy.start()
        sent.append(copy)
        return copy

    barrier = pltpu.get_barrier_semaphore()
    for step in range(1, n):
        pl.semaphore_signal(barrier, inc=1, device_id={"node": (me + step) % n})
    if paired:
        pl.semaphore_signal(barrier, inc=1, device_id={"member": other_member})
    loads = []
    for i, (source, target) in enumerate(zip(sources, locals_)):
        loads.append(pltpu.make_async_copy(source, target, in_sem.at[i]))

    def load(*which):
        for i in which:
            loads[i].start()

    def ready(*which):
        for i in which:
            loads[i].wait()

    load(2, 5, 6, 7)
    offsets, own = [0], []
    mine = y * 2 + core
    for k, shard in enumerate(shards):
        rows = shard.shape[0]
        target = w_ref.at[z, mine, pl.ds(offsets[k], rows), :]
        own.append(pltpu.make_async_copy(shard, target, own_sem.at[k]))
        own[k].start()
        offsets.append(offsets[k] + rows)
    load(0, 1, 3, 4, 9, 10, 8, 11, 12)

    groups = [(offsets[0], offsets[1]), (offsets[1], offsets[3]), (offsets[3], offsets[4]), (offsets[4], offsets[6])]
    near = x * part
    away = (1 - x) * part if paired else 0
    flights = {}

    def region(zz, lane, g, side):
        start, stop = groups[g]
        columns = pl.ds(pl.multiple_of(side, 128), part)
        return w_ref.at[zz, lane, pl.ds(start, stop - start), columns]

    def pass_core(g, i, zz, lane, side):
        spot = region(zz, lane, g, side)
        flights["c", g, i] = remote(spot, spot, c_send.at[g, i], c_recv.at[g, i], {"node": me + 1 - 2 * core})

    def pass_member(g, i, zz, lane):
        spot = region(zz, lane, g, near)
        flights["x", g, i] = remote(spot, spot, x_send.at[g, i], x_recv.at[g, i], {"member": other_member})

    def start_z(g):
        for j in range(1, deep):
            spot = region(z, mine, g, near)
            device = {"node": node_at((z + j) % deep, y, core)}
            flights["z", g, j] = remote(spot, spot, z_send.at[g, j], z_recv.at[g, j], device)

    every = pl.ds(0, deep)
    facing = (1 - y) * 2 + core

    def step_y(g):
        for j in range(1, deep):
            flights["z", g, j].wait_recv()
        if wide == 2:
            spot = region(every, mine, g, near)
            device = {"node": node_at(z, 1 - y, core)}
            flights["y", g] = remote(spot, spot, y_send.at[g], y_recv.at[g], device)
        if paired:
            for j in range(1, deep):
                pass_member(g, j, (z + j) % deep, mine)
        pass_core(g, 0, every, mine, near)

    def step_x(g):
        if wide == 2:
            flights["y", g].wait_recv()
            if paired:
                pass_member(g, 0, every, facing)
            pass_core(g, 1, every, facing, near)

    def step_c(g):
        if paired:
            for j in range(1, deep):
                flights["x", g, j].wait_recv()
            pass_core(g, 2, every, mine, away)
            if wide == 2:
                flights["x", g, 0].wait_recv()
                pass_core(g, 3, every, facing, away)

    def step_in(g):
        for i in range(4):
            if ("c", g, i) in flights:
                flights["c", g, i].wait_recv()

    def weight(k):
        return w_ref[:, :, offsets[k] : offsets[k + 1], :].reshape(-1, width)

    channels = embed_ref.shape[0]
    cap = rows_ref.shape[1]
    listed = n * cap
    points, fixed = cond_ref.shape[1], cond_ref.shape[0]
    frac = jnp.full((1, 1), step_ref[0], jnp.int32).astype(f32) / (STEPS - 1)
    upper = sigma_top ** (1.0 / rho_power)
    lower = sigma_low ** (1.0 / rho_power)
    root = upper + frac * (lower - upper)
    cube = root * root * root
    sigma = cube * cube * root
    turn_ref[...] = jnp.zeros_like(turn_ref)
    raw_ref[...] = jnp.zeros_like(raw_ref)
    ready(2)
    turn_ref[:n, :cap] = rows_ref[...].astype(f32)
    turned = turn_ref[...].T
    spots = lax.broadcasted_iota(jnp.int32, (cap, points), 1).astype(f32)
    for r in range(n):
        chosen = turned[:cap, r : r + 1] == spots
        pick_ref[r * cap : (r + 1) * cap, :] = chosen.astype(f32).astype(bf16)
    ready(5, 6, 7)
    raw_ref[:fixed, :] = cond_ref[...].astype(f32)
    raw_ref[fixed:channels, :] = (target_ref[...] + sigma * noise_ref[...]) / jnp.sqrt(sigma * sigma + 1.0)
    outgoing[...] = nt(pick_ref[...], raw_ref[...].astype(bf16)).astype(bf16).reshape(outgoing.shape)

    ready(4, 9)
    stack_left(mesh_s_ref, mesh_ref[...])
    stack_right(mesh_k_ref, mesh_w_ref[...])
    nodes_ref[...] = silu(nn(mesh_s_ref[...].T.astype(bf16), mesh_k_ref[...].astype(bf16))).astype(bf16)
    ready(3, 10)
    stack_left(geom_s_ref, geom_ref[...])
    stack_right(geom_k_ref, geom_w_ref[...])
    ready(0, 1)
    count = count_ref[0]
    nodes = mesh_ref.shape[1]
    blocks = geom_ref.shape[1] // block
    chunks = block // 128
    lanes = lax.broadcasted_iota(jnp.int32, (128, 128), 1).astype(f32)
    lane_row = lax.broadcasted_iota(jnp.int32, (1, 128), 1)
    node_rows = lax.broadcasted_iota(jnp.int32, (nodes, 128), 0).astype(f32)

    def prepare(b, carry):
        for c in range(chunks):
            j = b * chunks + c
            here = pl.ds(c * 128, 128)
            from_row = slot_ref[pl.ds(j, 1), :].astype(f32)
            to_row = jnp.where(j * 128 + lane_row < count, recv_ref[pl.ds(j, 1), :], -1).astype(f32)
            from_cols = jnp.broadcast_to(from_row, (128, 128)).T
            to_cols = jnp.broadcast_to(to_row, (128, 128)).T
            for t in range(listed // 128):
                ohs_ref[b, here, t * 128 : (t + 1) * 128] = (from_cols == lanes + 128.0 * t).astype(f32).astype(bf16)
            for t in range(nodes // 128):
                ohr_ref[here, t * 128 : (t + 1) * 128] = (to_cols == lanes + 128.0 * t).astype(f32).astype(bf16)
            place_ref[b, :, here] = (node_rows == to_row).astype(f32).astype(bf16)
        meshg_ref[b] = nn(ohr_ref[...], nodes_ref[...]).astype(bf16)
        here = pl.ds(pl.multiple_of(b * block, block), block)
        embedded = nn(geom_s_ref[:, here].T.astype(bf16), geom_k_ref[...].astype(bf16))
        edges_ref[b] = silu(embedded).astype(bf16)
        return carry

    def prepare_to(start, stop):
        lax.fori_loop(blocks * start // 8, blocks * stop // 8, prepare, 0)

    for copy in own:
        copy.wait()
    prepare_to(0, 2)
    pl.semaphore_wait(barrier, n if paired else n - 1)
    start_z(0)
    start_z(1)
    swaps = []
    for step in range(1, n):
        other = (me + step) % n
        swaps.append(
            remote(outgoing.at[other], arrived.at[me], a_send.at[step], a_recv.at[step], {"node": other})
        )
    start_z(2)
    start_z(3)
    stay = pltpu.make_async_copy(outgoing.at[me], arrived.at[me], own_sem.at[6])
    stay.start()
    prepare_to(2, 5)
    step_y(0)
    prepare_to(5, 6)
    step_y(1)
    step_x(0)
    prepare_to(6, 7)
    step_y(2)
    step_x(1)
    prepare_to(7, 8)
    step_c(0)
    step_x(2)

    ready(8, 11, 12)
    embed_pad_ref[...] = jnp.zeros_like(embed_pad_ref)
    embed_pad_ref[:channels, :] = embed_ref[...]
    freqs = noise_w_ref.shape[0] // 2
    place_k = lax.broadcasted_iota(jnp.int32, (2 * freqs, 1), 0)
    wave = (place_k % freqs + 1).astype(f32)
    angle = 0.25 * jnp.log(sigma) * wave
    fourier = jnp.where(place_k < freqs, jnp.sin(angle), jnp.cos(angle))
    cond = silu(jnp.sum(fourier * noise_w_ref[...], axis=0, keepdims=True)).astype(bf16)
    film = nn(cond, film_w_ref[...])
    edge_scale, edge_shift, node_scale, node_shift = [film[:, width * i : width * (i + 1)] for i in range(4)]
    stay.wait()
    for copy in swaps:
        copy.wait_recv()
    listing = arrived[...].reshape(listed, arrived.shape[2])
    received = silu(nn(listing, embed_pad_ref[...])).astype(bf16)
    step_c(1)
    step_in(0)

    def edge_part(i, carry):
        for u in range(2):
            pre_ref[2 * i + u] = nn(edges_ref[2 * i + u], weight(0))
        return carry

    lax.fori_loop(0, blocks // 4, edge_part, 0)
    step_c(2)
    step_y(3)
    step_in(1)
    lax.fori_loop(blocks // 4, blocks // 2, edge_part, 0)
    step_x(3)
    table_ref[...] = nn(received, weight(2)).astype(bf16)

    def hidden_part(i, carry):
        for u in range(2):
            b = 2 * i + u
            pre = pre_ref[b] + (nn(meshg_ref[b], weight(1)) + nn(ohs_ref[b], table_ref[...]))
            edges_ref[b] = silu(pre).astype(bf16)
        return carry

    lax.fori_loop(0, blocks // 2, hidden_part, 0)
    step_c(3)
    step_in(2)
    total_ref[...] = jnp.zeros_like(total_ref)
    mixed_ref[0] = nn(edges_ref[0], weight(3))
    for b in range(blocks):
        if b + 1 < blocks:
            mixed_ref[(b + 1) % 2] = nn(edges_ref[b + 1], weight(3))
        message = normalised(mixed_ref[b % 2]) * (1.0 + edge_scale) + edge_shift
        total_ref[...] += nn(place_ref[b], message.astype(bf16))
    step_in(3)
    joint = weight(5)
    update = nn(nodes_ref[...], joint[:width]) + nn(total_ref[...].astype(bf16), joint[width:])
    update = silu(update).astype(bf16)
    result = normalised(nn(update, weight(4))) * (1.0 + node_scale) + node_shift
    out_ref[...] = (nodes_ref[...].astype(f32) + result).astype(bf16)
    for copy in sent:
        copy.wait_send()


def per_device(n, members, folded, *args):
    conditioning, target_state, noise_sample, step_index, mesh_features, edge_geometry = args[:6]
    edge_slot, edge_receiver, send_rows, edge_count, embed_weight, mesh_weight, geom_weight = args[6:13]
    sender_w, edge_w, receiver_w, message_w, node_w, output_w = args[13:19]
    noise_weight, film_weight = args[19:]
    shards = (edge_w, receiver_w, sender_w, message_w, output_w, node_w)
    channels, width = embed_weight.shape
    nodes, edges = mesh_features.shape[1], edge_geometry.shape[1]
    cap = send_rows.shape[1]
    points = conditioning.shape[1]
    listed = n * cap
    deep = channels + -channels % 128
    block = min(512, edges)
    blocks = edges // block
    lines = 2 if folded else 1
    layers = n // 2 // lines
    stacked = sum(shard.shape[0] for shard in shards)
    inputs = (
        edge_slot.reshape(-1, 128),
        edge_receiver.reshape(-1, 128),
        send_rows,
        edge_geometry,
        mesh_features,
        conditioning,
        target_state,
        noise_sample,
        embed_weight,
        mesh_weight,
        geom_weight,
        noise_weight,
        film_weight,
    )
    dma = pltpu.SemaphoreType.DMA
    vmem = pl.BlockSpec(memory_space=pltpu.VMEM)
    smem = pl.BlockSpec(memory_space=pltpu.SMEM)
    hbm = pl.BlockSpec(memory_space=pltpu.HBM)
    return pl.pallas_call(
        functools.partial(encoder_kernel, n, members, folded, block),
        out_shape=jax.ShapeDtypeStruct((nodes, width), bf16),
        in_specs=[smem] * 2 + [hbm] * 19,
        out_specs=vmem,
        scratch_shapes=[pltpu.VMEM(value.shape, value.dtype) for value in inputs]
        + [
            pltpu.VMEM((layers, 2 * lines, stacked, width), bf16),
            pltpu.VMEM((deep, points), f32),
            pltpu.VMEM((listed, points), bf16),
            pltpu.VMEM((n, cap, deep), bf16),
            pltpu.VMEM((n, cap, deep), bf16),
            pltpu.VMEM((deep, width), bf16),
            pltpu.VMEM((128, 128), f32),
            pltpu.VMEM((128, nodes), f32),
            pltpu.VMEM((128, width), f32),
            pltpu.VMEM((128, edges), f32),
            pltpu.VMEM((128, width), f32),
            pltpu.VMEM((nodes, width), bf16),
            pltpu.VMEM((block, nodes), bf16),
            pltpu.VMEM((blocks, block, listed), bf16),
            pltpu.VMEM((blocks, nodes, block), bf16),
            pltpu.VMEM((blocks, block, width), bf16),
            pltpu.VMEM((blocks, block, width), bf16),
            pltpu.VMEM((blocks, block, width), f32),
            pltpu.VMEM((listed, width), bf16),
            pltpu.VMEM((2, block, width), f32),
            pltpu.VMEM((nodes, width), f32),
            dma((4, layers)),
            dma((4, layers)),
            dma((4,)),
            dma((4,)),
            dma((4, layers)),
            dma((4, layers)),
            dma((4, 4)),
            dma((4, 4)),
            dma((n,)),
            dma((n,)),
            dma((13,)),
            dma((7,)),
        ],
        compiler_params=pltpu.CompilerParams(
            collective_id=0, has_side_effects=True, vmem_limit_bytes=48 * 1024 * 1024
        ),
    )(step_index, edge_count, *inputs, *shards)


def solution(mesh):
    placed = (
        P(None, ("member", "node")),
        P(None, ("member", "node")),
        P(None, ("member", "node")),
        P("member"),
        P(None, "node"),
        P(None, "node"),
        P("node"),
        P("node"),
        P("node", None),
        P("node"),
        P(),
        P(),
        P(),
        P("node", None),
        P("node", None),
        P("node", None),
        P("node", None),
        P("node", None),
        P("node", None),
        P(),
        P(),
    )
    body = functools.partial(per_device, mesh.shape["node"], mesh.shape["member"], is_folded(mesh))
    return jax.shard_map(
        body, mesh=mesh, in_specs=placed, out_specs=P("node", "member"), check_vma=False
    )
```

time: 56.3 us -> 65.2 us (1.16); the launches traced: 56.1 us -> 64.2 us
  local copies, waits for them, and re-layouts: 3.31 us -> 16.8 us
  Pallas kernels: 51.4 us -> 46 us
    unnamed x1 -> x39, local copies, waits for them, and re-layouts: 1.97 us -> 16.8 us
    pallas_call x1, Pallas kernels: 51.4 us -> 46 us  [per_device(): pl.pallas_call(functools.partial(encoder_kernel, n, members, folded, bloc...]
    reshape x1 -> x0, local copies, waits for them, and re-layouts: 1.34 us -> none  [per_device(): send_rows.reshape(1, -1)]
where the time goes in v1:
time: 65.2 us; the launch traced here: 64.2 us
  Pallas kernels  46 us (71%)
  local copies, waits for them, and re-layouts  16.8 us (26%)
  between operations  1.33 us (2%)
    pallas_call x1, Pallas kernels, per_device(): pl.pallas_call(functools.partial(encoder_kernel, n, members, folded, bloc...  46 us
    unnamed x39, local copies, waits for them, and re-layouts  16.8 us

profile of v1, /device:TPU:0, one launch (start us, length us, event | category | flops | bytes accessed | tf_op | source)
XLA Modules:
  0.0 64.2 jit_solution(711396655492531994)
XLA Ops:
  1.3 0.0 copy-start
  1.3 1.6 %copy-done = bf16[512,2048]{1,0:T(8,128)(2,1)S(1)} copy-done((bf16[512,2048]{1,0:T(8,128)(2,1)S(1)}, bf16[512,2048]{1,0:T(8,128)(2,1)}, u32[]{:S(2)}) %copy-start) | copy-done | bytes 2097176
  2.9 0.0 copy-start.1
  2.9 1.0 %copy-done.1 = f32[84,1024]{1,0:T(8,128)S(1)} copy-done((f32[84,1024]{1,0:T(8,128)S(1)}, f32[84,1024]{1,0:T(8,128)}, u32[]{:S(2)}) %copy-start.1) | copy-done | bytes 344088
  3.9 0.0 copy-start.2
  3.9 1.0 %copy-done.2 = f32[84,1024]{1,0:T(8,128)S(1)} copy-done((f32[84,1024]{1,0:T(8,128)S(1)}, f32[84,1024]{1,0:T(8,128)}, u32[]{:S(2)}) %copy-start.2) | copy-done | bytes 344088
  4.9 1.0 %copy-done.3 = bf16[168,1024]{1,0:T(8,128)(2,1)S(1)} copy-done((bf16[168,1024]{1,0:T(8,128)(2,1)S(1)}, bf16[168,1024]{1,0:T(8,128)(2,1)}, u32[]{:S(2)}) %copy-start.3) | copy-done | bytes 344088
  5.8 0.9 %copy-done.4 = bf16[252,512]{1,0:T(8,128)(2,1)S(1)} copy-done((bf16[252,512]{1,0:T(8,128)(2,1)S(1)}, bf16[252,512]{1,0:T(8,128)(2,1)}, u32[]{:S(2)}) %copy-start.4) | copy-done | bytes 258072
  6.8 0.8 %copy-done.5 = f32[4,4096]{1,0:T(4,128)S(1)} copy-done((f32[4,4096]{1,0:T(4,128)S(1)}, f32[4,4096]{1,0:T(4,128)}, u32[]{:S(2)}) %copy-start.5) | copy-done | bytes 65560
  7.6 0.8 %copy-done.6 = f32[32,512]{1,0:T(8,128)S(1)} copy-done((f32[32,512]{1,0:T(8,128)S(1)}, f32[32,512]{1,0:T(8,128)}, u32[]{:S(2)}) %copy-start.6) | copy-done | bytes 65560
  8.5 0.8 %copy-done.7 = bf16[64,512]{1,0:T(8,128)(2,1)S(1)} copy-done((bf16[64,512]{1,0:T(8,128)(2,1)S(1)}, bf16[64,512]{1,0:T(8,128)(2,1)}, u32[]{:S(2)}) %copy-start.7) | copy-done | bytes 65560
  9.3 0.8 %copy-done.8 = bf16[32,512]{1,0:T(8,128)(2,1)S(1)} copy-done((bf16[32,512]{1,0:T(8,128)(2,1)S(1)}, bf16[32,512]{1,0:T(8,128)(2,1)}, u32[]{:S(2)}) %copy-start.8) | copy-done | bytes 32792
  10.1 0.8 %copy-done.9 = bf16[32,512]{1,0:T(8,128)(2,1)S(1)} copy-done((bf16[32,512]{1,0:T(8,128)(2,1)S(1)}, bf16[32,512]{1,0:T(8,128)(2,1)}, u32[]{:S(2)}) %copy-start.9) | copy-done | bytes 32792
  10.8 0.8 %copy-done.10 = bf16[32,512]{1,0:T(8,128)(2,1)S(1)} copy-done((bf16[32,512]{1,0:T(8,128)(2,1)S(1)}, bf16[32,512]{1,0:T(8,128)(2,1)}, u32[]{:S(2)}) %copy-start.10) | copy-done | bytes 32792
  11.6 0.8 %copy-done.11 = bf16[32,512]{1,0:T(8,128)(2,1)S(1)} copy-done((bf16[32,512]{1,0:T(8,128)(2,1)S(1)}, bf16[32,512]{1,0:T(8,128)(2,1)}, u32[]{:S(2)}) %copy-start.11) | copy-done | bytes 32792
  12.3 0.8 %copy-done.12 = bf16[32,512]{1,0:T(8,128)(2,1)S(1)} copy-done((bf16[32,512]{1,0:T(8,128)(2,1)S(1)}, bf16[32,512]{1,0:T(8,128)(2,1)}, u32[]{:S(2)}) %copy-start.12) | copy-done | bytes 32792
  13.1 0.7 %copy-done.13 = s32[4096]{0:T(1024)S(1)} copy-done((s32[4096]{0:T(1024)S(1)}, s32[4096]{0:T(1024)}, u32[]{:S(2)}) %copy-start.13) | copy-done | bytes 16408
  13.8 0.7 %copy-done.14 = s32[4096]{0:T(1024)S(1)} copy-done((s32[4096]{0:T(1024)S(1)}, s32[4096]{0:T(1024)}, u32[]{:S(2)}) %copy-start.14) | copy-done | bytes 16408
  14.5 0.7 %copy-done.15 = f32[3,640]{1,0:T(4,128)S(1)} copy-done((f32[3,640]{1,0:T(4,128)S(1)}, f32[3,640]{1,0:T(4,128)}, u32[]{:S(2)}) %copy-start.15) | copy-done | bytes 7704
  15.2 0.7 %copy-done.16 = s32[16,16]{1,0:T(8,128)S(1)} copy-done((s32[16,16]{1,0:T(8,128)S(1)}, s32[16,16]{1,0:T(8,128)}, u32[]{:S(2)}) %copy-start.16) | copy-done | bytes 1048
  15.9 0.7 %copy-done.17 = f32[3,512]{1,0:T(4,128)S(1)} copy-done((f32[3,512]{1,0:T(4,128)S(1)}, f32[3,512]{1,0:T(4,128)}, u32[]{:S(2)}) %copy-start.17) | copy-done | bytes 6168
  16.6 0.7 %copy-done.18 = f32[4,512]{1,0:T(4,128)S(1)} copy-done((f32[4,512]{1,0:T(4,128)S(1)}, f32[4,512]{1,0:T(4,128)}, u32[]{:S(2)}) %copy-start.18) | copy-done | bytes 8216
  17.3 46.0 %shard_map.199 = bf16[640,512]{1,0:T(8,128)(2,1)S(1)} custom-call(s32[1]{0:T(128)S(6)} %copy.23.refs_0_, s32[1]{0:T(128)S(6)} %copy.24.refs_1_, s32[32,128]{1,0:T(8,128)S(1)} %bitcast.2, s32[32,128]{1,0:T(8,128)S(1)} %bitcast.3, s32[16,16]{1,0:T(8,128)S(1)} %copy-done.16, f32[4,4096]{1,0:T(4,128)S(1)} %copy-done.5, f32[3,640]{1,0:T(4,128)S(1)} %copy-done.15, ...), custom_call_target="tpu_custom_call" | custom-call | tf_op jit(solution)/shard_map/pallas_call | solution.py:384
  63.3 0.8 %copy.25 = bf16[640,512]{1,0:T(8,128)(2,1)} copy(bf16[640,512]{1,0:T(8,128)(2,1)S(1)} %shard_map.199) | data formatting | bytes 1310720
  (16 shorter events, 0.0 us)
Async XLA Ops:
  1.3 1.6 %copy-start = (bf16[512,2048]{1,0:T(8,128)(2,1)S(1)}, bf16[512,2048]{1,0:T(8,128)(2,1)}, u32[]{:S(2)}) copy-start(bf16[512,2048]{1,0:T(8,128)(2,1)} %refs_14_.1) | copy-start | bytes 6291460
  2.9 1.0 %copy-start.1 = (f32[84,1024]{1,0:T(8,128)S(1)}, f32[84,1024]{1,0:T(8,128)}, u32[]{:S(2)}) copy-start(f32[84,1024]{1,0:T(8,128)} %refs_8_.1) | copy-start | bytes 1032196
  3.9 1.0 %copy-start.2 = (f32[84,1024]{1,0:T(8,128)S(1)}, f32[84,1024]{1,0:T(8,128)}, u32[]{:S(2)}) copy-start(f32[84,1024]{1,0:T(8,128)} %refs_9_.1) | copy-start | bytes 1032196
  4.9 1.0 %copy-start.3 = (bf16[168,1024]{1,0:T(8,128)(2,1)S(1)}, bf16[168,1024]{1,0:T(8,128)(2,1)}, u32[]{:S(2)}) copy-start(bf16[168,1024]{1,0:T(8,128)(2,1)} %refs_7_.1) | copy-start | bytes 1032196
  5.8 0.9 %copy-start.4 = (bf16[252,512]{1,0:T(8,128)(2,1)S(1)}, bf16[252,512]{1,0:T(8,128)(2,1)}, u32[]{:S(2)}) copy-start(bf16[252,512]{1,0:T(8,128)(2,1)} %refs_10_.1) | copy-start | bytes 774148
  6.8 0.8 %copy-start.5 = (f32[4,4096]{1,0:T(4,128)S(1)}, f32[4,4096]{1,0:T(4,128)}, u32[]{:S(2)}) copy-start(f32[4,4096]{1,0:T(4,128)} %refs_5_.1) | copy-start | bytes 196612
  7.6 0.8 %copy-start.6 = (f32[32,512]{1,0:T(8,128)S(1)}, f32[32,512]{1,0:T(8,128)}, u32[]{:S(2)}) copy-start(f32[32,512]{1,0:T(8,128)} %refs_13_.1) | copy-start | bytes 196612
  8.5 0.8 %copy-start.7 = (bf16[64,512]{1,0:T(8,128)(2,1)S(1)}, bf16[64,512]{1,0:T(8,128)(2,1)}, u32[]{:S(2)}) copy-start(bf16[64,512]{1,0:T(8,128)(2,1)} %refs_20_.1) | copy-start | bytes 196612
  9.3 0.8 %copy-start.8 = (bf16[32,512]{1,0:T(8,128)(2,1)S(1)}, bf16[32,512]{1,0:T(8,128)(2,1)}, u32[]{:S(2)}) copy-start(bf16[32,512]{1,0:T(8,128)(2,1)} %refs_15_.1) | copy-start | bytes 98308
  10.1 0.8 %copy-start.9 = (bf16[32,512]{1,0:T(8,128)(2,1)S(1)}, bf16[32,512]{1,0:T(8,128)(2,1)}, u32[]{:S(2)}) copy-start(bf16[32,512]{1,0:T(8,128)(2,1)} %refs_16_.1) | copy-start | bytes 98308
  10.8 0.8 %copy-start.10 = (bf16[32,512]{1,0:T(8,128)(2,1)S(1)}, bf16[32,512]{1,0:T(8,128)(2,1)}, u32[]{:S(2)}) copy-start(bf16[32,512]{1,0:T(8,128)(2,1)} %refs_17_.1) | copy-start | bytes 98308
  11.6 0.8 %copy-start.11 = (bf16[32,512]{1,0:T(8,128)(2,1)S(1)}, bf16[32,512]{1,0:T(8,128)(2,1)}, u32[]{:S(2)}) copy-start(bf16[32,512]{1,0:T(8,128)(2,1)} %refs_18_.1) | copy-start | bytes 98308
  12.3 0.8 %copy-start.12 = (bf16[32,512]{1,0:T(8,128)(2,1)S(1)}, bf16[32,512]{1,0:T(8,128)(2,1)}, u32[]{:S(2)}) copy-start(bf16[32,512]{1,0:T(8,128)(2,1)} %refs_19_.1) | copy-start | bytes 98308
  13.1 0.7 %copy-start.13 = (s32[4096]{0:T(1024)S(1)}, s32[4096]{0:T(1024)}, u32[]{:S(2)}) copy-start(s32[4096]{0:T(1024)} %param.27) | copy-start | bytes 49156
  13.8 0.7 %copy-start.14 = (s32[4096]{0:T(1024)S(1)}, s32[4096]{0:T(1024)}, u32[]{:S(2)}) copy-start(s32[4096]{0:T(1024)} %param.28) | copy-start | bytes 49156
  14.5 0.7 %copy-start.15 = (f32[3,640]{1,0:T(4,128)S(1)}, f32[3,640]{1,0:T(4,128)}, u32[]{:S(2)}) copy-start(f32[3,640]{1,0:T(4,128)} %refs_6_.1) | copy-start | bytes 23044
  15.2 0.7 %copy-start.16 = (s32[16,16]{1,0:T(8,128)S(1)}, s32[16,16]{1,0:T(8,128)}, u32[]{:S(2)}) copy-start(s32[16,16]{1,0:T(8,128)} %refs_4_.1) | copy-start | bytes 3076
  15.9 0.7 %copy-start.17 = (f32[3,512]{1,0:T(4,128)S(1)}, f32[3,512]{1,0:T(4,128)}, u32[]{:S(2)}) copy-start(f32[3,512]{1,0:T(4,128)} %refs_11_.1) | copy-start | bytes 18436
  16.6 0.7 %copy-start.18 = (f32[4,512]{1,0:T(4,128)S(1)}, f32[4,512]{1,0:T(4,128)}, u32[]{:S(2)}) copy-start(f32[4,512]{1,0:T(4,128)} %refs_12_.1) | copy-start | bytes 24580

commit v2 on v1

--- a/solution.py
+++ b/solution.py
@@ -78,8 +78,8 @@
     w_ref, raw_ref, pick_ref, outgoing, arrived, embed_pad_ref, turn_ref = refs[:7]
     mesh_s_ref, mesh_k_ref, geom_s_ref, geom_k_ref, nodes_ref, ohr_ref, ohs_ref = refs[7:14]
     place_ref, meshg_ref, edges_ref, pre_ref, table_ref, mixed_ref, total_ref = refs[14:21]
-    z_send, z_recv, y_send, y_recv, x_send, x_recv, c_send, c_recv = refs[21:29]
-    a_send, a_recv, in_sem, own_sem = refs[29:]
+    film_ref, received_ref = refs[21:23]
+    z_recv, y_recv, x_recv, f_recv, c_recv, a_recv, sent_sem, in_sem, own_sem, heard = refs[23:]
     me = lax.axis_index("node")
     member = lax.axis_index("member")
     wide = 2 if folded else 1
@@ -95,21 +95,24 @@
     def node_at(zz, yy, cc):
         return (zz * wide + yy) * 2 + cc
 
-    sent = []
-
-    def remote(source, target, send, recv, device):
+    def remote(source, target, way, recv, device):
         copy = pltpu.make_async_remote_copy(
-            src_ref=source, dst_ref=target, send_sem=send, recv_sem=recv, device_id=device
+            src_ref=source, dst_ref=target, send_sem=sent_sem.at[way], recv_sem=recv, device_id=device
         )
         copy.start()
-        sent.append(copy)
-        return copy
+
+    def arrive(like, sem):
+        pltpu.make_async_copy(like, like, sem).wait()
 
     barrier = pltpu.get_barrier_semaphore()
-    for step in range(1, n):
-        pl.semaphore_signal(barrier, inc=1, device_id={"node": (me + step) % n})
+    greeted = [{"node": node_at((z + j) % deep, y, core)} for j in range(1, deep)]
+    greeted.append({"node": me + 1 - 2 * core})
+    if wide == 2:
+        greeted.append({"node": node_at(z, 1 - y, core)})
     if paired:
-        pl.semaphore_signal(barrier, inc=1, device_id={"member": other_member})
+        greeted.append({"member": other_member})
+    for device in greeted:
+        pl.semaphore_signal(barrier, inc=1, device_id=device)
     loads = []
     for i, (source, target) in enumerate(zip(sources, locals_)):
         loads.append(pltpu.make_async_copy(source, target, in_sem.at[i]))
@@ -123,75 +126,72 @@
             loads[i].wait()
 
     load(2, 5, 6, 7)
-    offsets, own = [0], []
+    offsets = [0]
     mine = y * 2 + core
-    for k, shard in enumerate(shards):
+    for shard in shards:
         rows = shard.shape[0]
-        target = w_ref.at[z, mine, pl.ds(offsets[k], rows), :]
-        own.append(pltpu.make_async_copy(shard, target, own_sem.at[k]))
-        own[k].start()
-        offsets.append(offsets[k] + rows)
+        target = w_ref.at[z, mine, pl.ds(offsets[-1], rows), :]
+        pltpu.make_async_copy(shard, target, own_sem).start()
+        offsets.append(offsets[-1] + rows)
     load(0, 1, 3, 4, 9, 10, 8, 11, 12)
 
-    groups = [(offsets[0], offsets[1]), (offsets[1], offsets[3]), (offsets[3], offsets[4]), (offsets[4], offsets[6])]
+    groups = [(offsets[k], offsets[k + 1]) for k in range(6)]
     near = x * part
     away = (1 - x) * part if paired else 0
-    flights = {}
+    whole = ()
+    every, others = pl.ds(0, deep), pl.ds(0, deep - 1)
+    facing = (1 - y) * 2 + core
+    partner = {"node": me + 1 - 2 * core}
+
+    def halved(g):
+        return paired and g not in whole
 
     def region(zz, lane, g, side):
         start, stop = groups[g]
+        if not halved(g):
+            return w_ref.at[zz, lane, pl.ds(start, stop - start), :]
         columns = pl.ds(pl.multiple_of(side, 128), part)
         return w_ref.at[zz, lane, pl.ds(start, stop - start), columns]
 
-    def pass_core(g, i, zz, lane, side):
-        spot = region(zz, lane, g, side)
-        flights["c", g, i] = remote(spot, spot, c_send.at[g, i], c_recv.at[g, i], {"node": me + 1 - 2 * core})
-
-    def pass_member(g, i, zz, lane):
-        spot = region(zz, lane, g, near)
-        flights["x", g, i] = remote(spot, spot, x_send.at[g, i], x_recv.at[g, i], {"member": other_member})
+    def pass_core(g, lane, side):
+        spot = region(every, lane, g, side)
+        remote(spot, spot, 4, c_recv.at[g], partner)
 
     def start_z(g):
         for j in range(1, deep):
             spot = region(z, mine, g, near)
-            device = {"node": node_at((z + j) % deep, y, core)}
-            flights["z", g, j] = remote(spot, spot, z_send.at[g, j], z_recv.at[g, j], device)
-
-    every = pl.ds(0, deep)
-    facing = (1 - y) * 2 + core
+            remote(spot, spot, 0, z_recv.at[g], {"node": node_at((z + j) % deep, y, core)})
 
     def step_y(g):
-        for j in range(1, deep):
-            flights["z", g, j].wait_recv()
+        arrive(region(others, mine, g, near), z_recv.at[g])
         if wide == 2:
             spot = region(every, mine, g, near)
-            device = {"node": node_at(z, 1 - y, core)}
-            flights["y", g] = remote(spot, spot, y_send.at[g], y_recv.at[g], device)
-        if paired:
+            remote(spot, spot, 1, y_recv.at[g], {"node": node_at(z, 1 - y, core)})
+        if halved(g):
             for j in range(1, deep):
-                pass_member(g, j, (z + j) % deep, mine)
-        pass_core(g, 0, every, mine, near)
+                spot = region((z + j) % deep, mine, g, near)
+                remote(spot, spot, 2, x_recv.at[g], {"member": other_member})
+        pass_core(g, mine, near)
 
     def step_x(g):
         if wide == 2:
-            flights["y", g].wait_recv()
-            if paired:
-                pass_member(g, 0, every, facing)
-            pass_core(g, 1, every, facing, near)
+            spot = region(every, facing, g, near)
+            arrive(spot, y_recv.at[g])
+            if halved(g):
+                remote(spot, spot, 3, f_recv.at[g], {"member": other_member})
+            pass_core(g, facing, near)
 
     def step_c(g):
-        if paired:
-            for j in range(1, deep):
-                flights["x", g, j].wait_recv()
-            pass_core(g, 2, every, mine, away)
+        if halved(g):
+            arrive(region(others, mine, g, away), x_recv.at[g])
+            pass_core(g, mine, away)
             if wide == 2:
-                flights["x", g, 0].wait_recv()
-                pass_core(g, 3, every, facing, away)
+                arrive(region(every, facing, g, away), f_recv.at[g])
+                pass_core(g, facing, away)
 
     def step_in(g):
-        for i in range(4):
-            if ("c", g, i) in flights:
-                flights["c", g, i].wait_recv()
+        start, stop = groups[g]
+        arrive(w_ref.at[:, pl.ds(0, wide), pl.ds(start, stop - start), :], c_recv.at[g])
 
     def weight(k):
         return w_ref[:, :, offsets[k] : offsets[k + 1], :].reshape(-1, width)
@@ -206,28 +206,31 @@
     root = upper + frac * (lower - upper)
     cube = root * root * root
     sigma = cube * cube * root
-    turn_ref[...] = jnp.zeros_like(turn_ref)
-    raw_ref[...] = jnp.zeros_like(raw_ref)
-    ready(2)
-    turn_ref[:n, :cap] = rows_ref[...].astype(f32)
-    turned = turn_ref[...].T
-    spots = lax.broadcasted_iota(jnp.int32, (cap, points), 1).astype(f32)
-    for r in range(n):
-        chosen = turned[:cap, r : r + 1] == spots
-        pick_ref[r * cap : (r + 1) * cap, :] = chosen.astype(f32).astype(bf16)
-    ready(5, 6, 7)
-    raw_ref[:fixed, :] = cond_ref[...].astype(f32)
-    raw_ref[fixed:channels, :] = (target_ref[...] + sigma * noise_ref[...]) / jnp.sqrt(sigma * sigma + 1.0)
-    outgoing[...] = nt(pick_ref[...], raw_ref[...].astype(bf16)).astype(bf16).reshape(outgoing.shape)
-
-    ready(4, 9)
-    stack_left(mesh_s_ref, mesh_ref[...])
-    stack_right(mesh_k_ref, mesh_w_ref[...])
-    nodes_ref[...] = silu(nn(mesh_s_ref[...].T.astype(bf16), mesh_k_ref[...].astype(bf16))).astype(bf16)
-    ready(3, 10)
-    stack_left(geom_s_ref, geom_ref[...])
-    stack_right(geom_k_ref, geom_w_ref[...])
-    ready(0, 1)
+    def make_picks():
+        turn_ref[...] = jnp.zeros_like(turn_ref)
+        raw_ref[...] = jnp.zeros_like(raw_ref)
+        ready(2)
+        turn_ref[:n, :cap] = rows_ref[...].astype(f32)
+        turned = turn_ref[...].T
+        spots = lax.broadcasted_iota(jnp.int32, (cap, points), 1).astype(f32)
+        for r in range(n):
+            chosen = turned[:cap, r : r + 1] == spots
+            pick_ref[r * cap : (r + 1) * cap, :] = chosen.astype(f32).astype(bf16)
+        ready(5, 6, 7)
+        raw_ref[:fixed, :] = cond_ref[...].astype(f32)
+        raw_ref[fixed:channels, :] = (target_ref[...] + sigma * noise_ref[...]) / jnp.sqrt(sigma * sigma + 1.0)
+        outgoing[...] = nt(pick_ref[...], raw_ref[...].astype(bf16)).astype(bf16).reshape(outgoing.shape)
+
+    def make_nodes():
+        ready(4, 9)
+        stack_left(mesh_s_ref, mesh_ref[...])
+        stack_right(mesh_k_ref, mesh_w_ref[...])
+        nodes_ref[...] = silu(nn(mesh_s_ref[...].T.astype(bf16), mesh_k_ref[...].astype(bf16))).astype(bf16)
+        ready(3, 10)
+        stack_left(geom_s_ref, geom_ref[...])
+        stack_right(geom_k_ref, geom_w_ref[...])
+        ready(0, 1)
+
     count = count_ref[0]
     nodes = mesh_ref.shape[1]
     blocks = geom_ref.shape[1] // block
@@ -258,91 +261,167 @@
     def prepare_to(start, stop):
         lax.fori_loop(blocks * start // 8, blocks * stop // 8, prepare, 0)
 
-    for copy in own:
-        copy.wait()
-    prepare_to(0, 2)
-    pl.semaphore_wait(barrier, n if paired else n - 1)
+    def start_exchange():
+        for step in range(1, n):
+            other = (me + step) % n
+            remote(outgoing.at[other], arrived.at[me], 5, a_recv, {"node": other})
+
+    stay = pltpu.make_async_copy(outgoing.at[me], arrived.at[me], in_sem.at[2])
+
+    def start_local(_, carry):
+        make_picks()
+        make_nodes()
+        return carry
+
+    def end_exchange():
+        stay.wait()
+        arrive(arrived.at[pl.ds(0, n - 1)], a_recv)
+
+    def prepare_noise():
+        ready(11, 12)
+        freqs = noise_w_ref.shape[0] // 2
+        place_k = lax.broadcasted_iota(jnp.int32, (2 * freqs, 1), 0)
+        wave = (place_k % freqs + 1).astype(f32)
+        angle = 0.25 * jnp.log(sigma) * wave
+        fourier = jnp.where(place_k < freqs, jnp.sin(angle), jnp.cos(angle))
+        cond = silu(jnp.sum(fourier * noise_w_ref[...], axis=0, keepdims=True)).astype(bf16)
+        film = nn(cond, film_w_ref[...])
+        film_ref[...] = film
+        ready(8)
+        embed_pad_ref[...] = jnp.zeros_like(embed_pad_ref)
+        embed_pad_ref[:channels, :] = embed_ref[...]
+
+    def receive():
+        end_exchange()
+        listing = arrived[...].reshape(listed, arrived.shape[2])
+        received_ref[...] = silu(nn(listing, embed_pad_ref[...])).astype(bf16)
+
+    def rows_of(b):
+        return pl.ds(pl.multiple_of(b * block, block), block)
+
+    def edge_part(b, carry):
+        pre_ref[rows_of(b), :] = nn(edges_ref[b], weight(0))
+        return carry
+
+    def node_part(b, carry):
+        pre_ref[rows_of(b), :] += nn(meshg_ref[b], weight(1))
+        return carry
+
+    def make_table():
+        table_ref[...] = nn(received_ref[...], weight(2)).astype(bf16)
+
+    def hidden_part(b, carry):
+        pre = pre_ref[rows_of(b), :] + nn(ohs_ref[b], table_ref[...])
+        edges_ref[b] = silu(pre).astype(bf16)
+        return carry
+
+    def film_row(k):
+        return film_ref[:, width * k : width * (k + 1)]
+
+    def mix(b):
+        mixed_ref[b % 2] = nn(edges_ref[b], weight(3))
+
+    def message_part(b):
+        if b + 1 < blocks:
+            mix(b + 1)
+        message = normalised(mixed_ref[b % 2]) * (1.0 + film_row(0)) + film_row(1)
+        total_ref[...] += nn(place_ref[b], message.astype(bf16))
+
+    def loop(body, start, stop, unroll=2):
+        first, last = blocks * start // 8, blocks * stop // 8
+        unroll = min(unroll, last - first)
+        if (last - first) % unroll:
+            unroll = 1
+
+        def several(i, carry):
+            for u in range(unroll):
+                body(first + unroll * i + u, carry)
+            return carry
+
+        lax.fori_loop(0, (last - first) // unroll, several, 0)
+
+    arrive(w_ref.at[z, mine], own_sem)
+    pl.semaphore_wait(barrier, len(greeted))
+    pl.semaphore_signal(heard.at[0], inc=1, device_id=partner)
     start_z(0)
     start_z(1)
-    swaps = []
-    for step in range(1, n):
-        other = (me + step) % n
-        swaps.append(
-            remote(outgoing.at[other], arrived.at[me], a_send.at[step], a_recv.at[step], {"node": other})
-        )
     start_z(2)
     start_z(3)
-    stay = pltpu.make_async_copy(outgoing.at[me], arrived.at[me], own_sem.at[6])
+    pl.semaphore_wait(heard.at[0], 1)
+    if wide == 2:
+        pl.semaphore_signal(heard.at[1], inc=1, device_id={"node": node_at(z, 1 - y, core)})
+    make_picks()
+    if wide == 2:
+        pl.semaphore_wait(heard.at[1], 1)
+    start_exchange()
     stay.start()
-    prepare_to(2, 5)
+    start_z(5)
+    start_z(4)
+    make_nodes()
     step_y(0)
-    prepare_to(5, 6)
+    loop(prepare, 0, 1, 1)
     step_y(1)
+    loop(prepare, 1, 2, 1)
     step_x(0)
-    prepare_to(6, 7)
     step_y(2)
+    loop(prepare, 2, 3, 1)
     step_x(1)
-    prepare_to(7, 8)
+    loop(prepare, 3, 4, 1)
+    step_y(3)
+    loop(prepare, 4, 5, 1)
+    step_x(2)
+    loop(prepare, 5, 6, 1)
     step_c(0)
-    step_x(2)
-
-    ready(8, 11, 12)
-    embed_pad_ref[...] = jnp.zeros_like(embed_pad_ref)
-    embed_pad_ref[:channels, :] = embed_ref[...]
-    freqs = noise_w_ref.shape[0] // 2
-    place_k = lax.broadcasted_iota(jnp.int32, (2 * freqs, 1), 0)
-    wave = (place_k % freqs + 1).astype(f32)
-    angle = 0.25 * jnp.log(sigma) * wave
-    fourier = jnp.where(place_k < freqs, jnp.sin(angle), jnp.cos(angle))
-    cond = silu(jnp.sum(fourier * noise_w_ref[...], axis=0, keepdims=True)).astype(bf16)
-    film = nn(cond, film_w_ref[...])
-    edge_scale, edge_shift, node_scale, node_shift = [film[:, width * i : width * (i + 1)] for i in range(4)]
-    stay.wait()
-    for copy in swaps:
-        copy.wait_recv()
-    listing = arrived[...].reshape(listed, arrived.shape[2])
-    received = silu(nn(listing, embed_pad_ref[...])).astype(bf16)
+    step_x(3)
+    loop(prepare, 6, 7, 1)
     step_c(1)
+    loop(prepare, 7, 8, 1)
     step_in(0)
-
-    def edge_part(i, carry):
-        for u in range(2):
-            pre_ref[2 * i + u] = nn(edges_ref[2 * i + u], weight(0))
-        return carry
-
-    lax.fori_loop(0, blocks // 4, edge_part, 0)
+    step_y(5)
+    loop(edge_part, 0, 4, 8)
     step_c(2)
-    step_y(3)
+    loop(edge_part, 4, 8, 8)
+    prepare_noise()
     step_in(1)
-    lax.fori_loop(blocks // 4, blocks // 2, edge_part, 0)
-    step_x(3)
-    table_ref[...] = nn(received, weight(2)).astype(bf16)
-
-    def hidden_part(i, carry):
-        for u in range(2):
-            b = 2 * i + u
-            pre = pre_ref[b] + (nn(meshg_ref[b], weight(1)) + nn(ohs_ref[b], table_ref[...]))
-            edges_ref[b] = silu(pre).astype(bf16)
-        return carry
-
-    lax.fori_loop(0, blocks // 2, hidden_part, 0)
+    loop(node_part, 0, 4, 8)
     step_c(3)
+    step_x(5)
+    loop(node_part, 4, 8, 8)
+    receive()
+    step_y(4)
     step_in(2)
+    make_table()
+    loop(hidden_part, 0, 4, 8)
+    step_x(4)
+    loop(hidden_part, 4, 8, 8)
+    step_in(3)
     total_ref[...] = jnp.zeros_like(total_ref)
-    mixed_ref[0] = nn(edges_ref[0], weight(3))
-    for b in range(blocks):
-        if b + 1 < blocks:
-            mixed_ref[(b + 1) % 2] = nn(edges_ref[b + 1], weight(3))
-        message = normalised(mixed_ref[b % 2]) * (1.0 + edge_scale) + edge_shift
-        total_ref[...] += nn(place_ref[b], message.astype(bf16))
-    step_in(3)
+    mix(0)
+    for b in range(blocks * 0 // 8, blocks * 2 // 8):
+        message_part(b)
+    step_c(5)
+    for b in range(blocks * 2 // 8, blocks * 4 // 8):
+        message_part(b)
+    step_c(4)
+    for b in range(blocks * 4 // 8, blocks * 8 // 8):
+        message_part(b)
+    step_in(5)
+    step_in(4)
     joint = weight(5)
     update = nn(nodes_ref[...], joint[:width]) + nn(total_ref[...].astype(bf16), joint[width:])
     update = silu(update).astype(bf16)
-    result = normalised(nn(update, weight(4))) * (1.0 + node_scale) + node_shift
+    result = normalised(nn(update, weight(4))) * (1.0 + film_row(2)) + film_row(3)
     out_ref[...] = (nodes_ref[...].astype(f32) + result).astype(bf16)
-    for copy in sent:
-        copy.wait_send()
+    for g in range(6):
+        arrive(region(others, mine, g, near), sent_sem.at[0])
+        if wide == 2:
+            arrive(region(every, mine, g, near), sent_sem.at[1])
+        if halved(g):
+            arrive(region(others, mine, g, near), sent_sem.at[2])
+            if wide == 2:
+                arrive(region(every, mine, g, near), sent_sem.at[3])
+    arrive(w_ref.at[:, pl.ds(0, wide), :, :], sent_sem.at[4])
+    arrive(arrived.at[pl.ds(0, n - 1)], sent_sem.at[5])
 
 
 def per_device(n, members, folded, *args):
@@ -405,26 +484,24 @@
             pltpu.VMEM((blocks, nodes, block), bf16),
             pltpu.VMEM((blocks, block, width), bf16),
             pltpu.VMEM((blocks, block, width), bf16),
-            pltpu.VMEM((blocks, block, width), f32),
+            pltpu.VMEM((edges, width), f32),
             pltpu.VMEM((listed, width), bf16),
             pltpu.VMEM((2, block, width), f32),
             pltpu.VMEM((nodes, width), f32),
-            dma((4, layers)),
-            dma((4, layers)),
-            dma((4,)),
-            dma((4,)),
-            dma((4, layers)),
-            dma((4, layers)),
-            dma((4, 4)),
-            dma((4, 4)),
-            dma((n,)),
-            dma((n,)),
+            pltpu.VMEM((1, 4 * width), f32),
+            pltpu.VMEM((listed, width), bf16),
+            dma((6,)),
+            dma((6,)),
+            dma((6,)),
+            dma((6,)),
+            dma((6,)),
+            dma,
+            dma((6,)),
             dma((13,)),
-            dma((7,)),
+            dma,
+            pltpu.SemaphoreType.REGULAR((2,)),
         ],
-        compiler_params=pltpu.CompilerParams(
-            collective_id=0, has_side_effects=True, vmem_limit_bytes=48 * 1024 * 1024
-        ),
+        compiler_params=pltpu.CompilerParams(collective_id=0, has_side_effects=True),
     )(step_index, edge_count, *inputs, *shards)
 
 

time: 65.2 us -> 43.6 us (0.67); the launches traced: 64.2 us -> 43.5 us
  local copies, waits for them, and re-layouts: 16.8 us -> 1.97 us
  Pallas kernels: 46 us -> 40.2 us
    unnamed x39 -> x1, local copies, waits for them, and re-layouts: 16.8 us -> 1.97 us
    pallas_call x1, Pallas kernels: 46 us -> 40.2 us  [per_device(): pl.pallas_call(functools.partial(encoder_kernel, n, members, folded, bloc...]
where the time goes in v2:
time: 43.6 us; the launch traced here: 43.5 us
  Pallas kernels  40.2 us (92%)
  local copies, waits for them, and re-layouts  1.97 us (5%)
  between operations  1.31 us (3%)
    pallas_call x1, Pallas kernels, per_device(): pl.pallas_call(functools.partial(encoder_kernel, n, members, folded, bloc...  40.2 us
    unnamed x1, local copies, waits for them, and re-layouts  1.97 us

profile of v2, /device:TPU:0, one launch (start us, length us, event | category | flops | bytes accessed | tf_op | source)
XLA Modules:
  0.0 43.5 jit_solution(17284989788566942163)
XLA Ops:
  1.3 40.2 %shard_map.199 = bf16[640,512]{1,0:T(8,128)(2,1)} custom-call(s32[1]{0:T(128)S(6)} %copy.23.refs_0_, s32[1]{0:T(128)S(6)} %copy.24.refs_1_, s32[32,128]{1,0:T(8,128)} %bitcast.2, s32[32,128]{1,0:T(8,128)} %bitcast.3, s32[16,16]{1,0:T(8,128)} %refs_4_.1, f32[4,4096]{1,0:T(4,128)} %refs_5_.1, f32[3,640]{1,0:T(4,128)} %refs_6_.1, bf16[168,1024]{1,0:T(8,128)(2,1)} %refs_7_.1, ...), custom_call_target="tpu_custom_call" | custom-call | tf_op jit(solution)/shard_map/pallas_call | solution.py:463
  41.5 2.0 %copy.25 = bf16[640,512]{1,0:T(8,128)(2,1)} copy(bf16[640,512]{1,0:T(8,128)(2,1)} %shard_map.199) | data formatting | bytes 1310720

commit v3 on v2

--- a/solution.py
+++ b/solution.py
@@ -366,34 +366,32 @@
     step_y(2)
     loop(prepare, 2, 3, 1)
     step_x(1)
+    prepare_noise()
+    step_y(3)
     loop(prepare, 3, 4, 1)
-    step_y(3)
+    step_x(2)
     loop(prepare, 4, 5, 1)
-    step_x(2)
-    loop(prepare, 5, 6, 1)
     step_c(0)
     step_x(3)
+    loop(prepare, 5, 6, 1)
+    step_c(1)
     loop(prepare, 6, 7, 1)
-    step_c(1)
+    receive()
+    step_y(5)
     loop(prepare, 7, 8, 1)
     step_in(0)
-    step_y(5)
     loop(edge_part, 0, 4, 8)
     step_c(2)
+    step_y(4)
     loop(edge_part, 4, 8, 8)
-    prepare_noise()
+    step_x(5)
     step_in(1)
-    loop(node_part, 0, 4, 8)
     step_c(3)
-    step_x(5)
-    loop(node_part, 4, 8, 8)
-    receive()
-    step_y(4)
+    loop(node_part, 0, 8, 8)
+    step_x(4)
     step_in(2)
     make_table()
-    loop(hidden_part, 0, 4, 8)
-    step_x(4)
-    loop(hidden_part, 4, 8, 8)
+    loop(hidden_part, 0, 8, 8)
     step_in(3)
     total_ref[...] = jnp.zeros_like(total_ref)
     mix(0)

time: 43.6 us -> 42 us (0.963)
  Pallas kernels: 40.2 us -> 38.6 us
    pallas_call x1, Pallas kernels: 40.2 us -> 38.6 us  [per_device(): pl.pallas_call(functools.partial(encoder_kernel, n, members, folded, bloc...]
where the time goes in v3:
time: 42 us; the launch traced here: 41.8 us
  Pallas kernels  38.6 us (92%)
  local copies, waits for them, and re-layouts  1.97 us (5%)
  between operations  1.31 us (3%)
    pallas_call x1, Pallas kernels, per_device(): pl.pallas_call(functools.partial(encoder_kernel, n, members, folded, bloc...  38.6 us
    unnamed x1, local copies, waits for them, and re-layouts  1.97 us

profile of v3, /device:TPU:0, one launch (start us, length us, event | category | flops | bytes accessed | tf_op | source)
XLA Modules:
  0.0 41.8 jit_solution(8485352481765136614)
XLA Ops:
  1.3 38.6 %shard_map.199 = bf16[640,512]{1,0:T(8,128)(2,1)} custom-call(s32[1]{0:T(128)S(6)} %copy.23.refs_0_, s32[1]{0:T(128)S(6)} %copy.24.refs_1_, s32[32,128]{1,0:T(8,128)} %bitcast.2, s32[32,128]{1,0:T(8,128)} %bitcast.3, s32[16,16]{1,0:T(8,128)} %refs_4_.1, f32[4,4096]{1,0:T(4,128)} %refs_5_.1, f32[3,640]{1,0:T(4,128)} %refs_6_.1, bf16[168,1024]{1,0:T(8,128)(2,1)} %refs_7_.1, ...), custom_call_target="tpu_custom_call" | custom-call | tf_op jit(solution)/shard_map/pallas_call | solution.py:461
  39.9 2.0 %copy.25 = bf16[640,512]{1,0:T(8,128)(2,1)} copy(bf16[640,512]{1,0:T(8,128)(2,1)} %shard_map.199) | data formatting | bytes 1310720
